TPU v7x, 32 devices: a whole 2x2x4 slice. The times are simulated.
32 devices in a mesh: slab: 8 (over z, x), yz: 4 (over y, core).
Axes of the slice: x: 2, y: 2, z: 4, core: 2. Of those that a mesh axis runs over, the one named last changes fastest.
Arguments:
- embeddings: bfloat16 [512, 25, 128], P(('slab', 'yz')), may hold values from -6 to 6
- neighbours: int32 [16384], P(('slab', 'yz')), may hold values from 0 to 127
- valid: int32 [16384], P(('slab', 'yz')), may hold values 0 or 1
- azimuth: float32 [16384], P(('slab', 'yz')), may hold values from -3.140625 to 3.140625
- polar: float32 [16384], P(('slab', 'yz')), may hold values from 0 to 3.14159
- distance: float32 [16384], P(('slab', 'yz')), may hold values from 0.9 to 5
- send_low: int32 [256], P(('slab', 'yz')), may hold values from 0 to 15
- send_high: int32 [256], P(('slab', 'yz')), may hold values from 0 to 15
- w_zero: bfloat16 [2, 640, 640], replicated, may hold values from -0.25 to 0.25
- w_one_re: bfloat16 [2, 512, 512], replicated, may hold values from -0.25 to 0.25
- w_one_im: bfloat16 [2, 512, 512], replicated, may hold values from -0.25 to 0.25
- w_two_re: bfloat16 [2, 384, 384], replicated, may hold values from -0.3125 to 0.3125
- w_two_im: bfloat16 [2, 384, 384], replicated, may hold values from -0.3125 to 0.3125
- radial_weight: float32 [2, 8, 128], replicated, may hold values from -2 to 2
- readout: float32 [128], replicated, may hold values from -0.5 to 0.5
Outputs:
- updated: bfloat16 [512, 25, 128], P(('slab', 'yz'))
- forces: float32 [3, 512], P(None, ('slab', 'yz'))
All inputs are finite; a program needn't handle non-finite values. No bound on the sum of `valid` on one device may be relied on, other than what follows from the above.
Results may differ from a plain program's by a relative error of at most 0.0043.
Values may be sent and summed in bfloat16 or wider, within the bound.
A program may use at most 64 MiB of HBM per device.

v0:
```python
import math

import jax
import jax.numpy as jnp
from jax import lax
from jax.sharding import PartitionSpec as P

NEIGHB = 32
LAYERS = 2


HIGHEST = lax.Precision.HIGHEST


def from_behind(block, axis, distance):
    devices = range(lax.axis_size(axis))
    route = [((i - distance) % len(devices), i) for i in devices]
    return lax.ppermute(block, axis, route)


def slot_index(degree, azimuth_order):
    return degree * degree + degree + azimuth_order


def radial_scale(distance, radial_weight):
    centers = 1.0 + 0.5 * jnp.arange(8, dtype=jnp.float32)
    basis_values = jnp.exp(-jnp.square((distance[:, None] - centers[None, :]) / 0.5))
    return jax.nn.silu(jnp.dot(basis_values, radial_weight, precision=HIGHEST))


def slot_groups(degrees):
    zero_slots = [slot_index(degree, 0) for degree in range(degrees)]
    groups = [zero_slots]
    for azimuth_order in (1, 2):
        groups.append(
            [slot_index(degree, azimuth_order) for degree in range(azimuth_order, degrees)]
        )
        groups.append(
            [slot_index(degree, -azimuth_order) for degree in range(azimuth_order, degrees)]
        )
    return groups


def grouped_rows(rows, degrees):
    order = [coeff_slot for group in slot_groups(degrees) for coeff_slot in group]
    return jnp.concatenate([rows[:, coeff_slot] for coeff_slot in order], axis=1)


def convolve(
    features,
    degrees,
    channel_count,
    azimuth,
    distance,
    valid,
    w_zero,
    w_one_re,
    w_one_im,
    w_two_re,
    w_two_im,
    radial_weight,
):
    edge_count = features.shape[0]
    atom_count = edge_count // NEIGHB
    radial = radial_scale(distance, radial_weight) * valid.astype(jnp.float32)[:, None]
    radial_rows = radial[:, None, :]
    groups = slot_groups(degrees)
    bounds = []
    offset = 0
    for group in groups:
        bounds.append((offset, offset + len(group) * channel_count))
        offset += len(group) * channel_count
    results = [None] * (degrees * degrees)
    zero_in = features[:, bounds[0][0] : bounds[0][1]]
    zero_out = (
        jnp.dot(zero_in, w_zero, preferred_element_type=jnp.float32).reshape(
            edge_count, degrees, channel_count
        )
        * radial_rows
    )
    zero_sum = zero_out.reshape(atom_count, NEIGHB, degrees, channel_count).sum(axis=1)
    for position, coeff_slot in enumerate(groups[0]):
        results[coeff_slot] = zero_sum[:, position]
    for index_pair, azimuth_order, real_part, imag_part in (
        (1, 1, w_one_re, w_one_im),
        (3, 2, w_two_re, w_two_im),
    ):
        plus_slots = groups[index_pair]
        minus_slots = groups[index_pair + 1]
        plus_part = features[:, bounds[index_pair][0] : bounds[index_pair][1]].astype(jnp.float32)
        minus_part = features[:, bounds[index_pair + 1][0] : bounds[index_pair + 1][1]].astype(
            jnp.float32
        )
        cosine = jnp.cos(azimuth_order * azimuth)[:, None]
        sine = jnp.sin(azimuth_order * azimuth)[:, None]
        turned_plus = (cosine * plus_part + sine * minus_part).astype(jnp.bfloat16)
        turned_minus = (cosine * minus_part - sine * plus_part).astype(jnp.bfloat16)
        count = len(plus_slots)
        out_plus = (
            jnp.dot(turned_plus, real_part, preferred_element_type=jnp.float32)
            - jnp.dot(turned_minus, imag_part, preferred_element_type=jnp.float32)
        ).reshape(edge_count, count, channel_count) * radial_rows
        out_minus = (
            jnp.dot(turned_plus, imag_part, preferred_element_type=jnp.float32)
            + jnp.dot(turned_minus, real_part, preferred_element_type=jnp.float32)
        ).reshape(edge_count, count, channel_count) * radial_rows
        cos_rows = cosine[:, :, None]
        sin_rows = sine[:, :, None]
        back_plus = (
            (cos_rows * out_plus - sin_rows * out_minus)
            .reshape(atom_count, NEIGHB, count, channel_count)
            .sum(axis=1)
        )
        back_minus = (
            (sin_rows * out_plus + cos_rows * out_minus)
            .reshape(atom_count, NEIGHB, count, channel_count)
            .sum(axis=1)
        )
        for position, coeff_slot in enumerate(plus_slots):
            results[coeff_slot] = back_plus[:, position]
        for position, coeff_slot in enumerate(minus_slots):
            results[coeff_slot] = back_minus[:, position]
    blank = jnp.zeros((atom_count, channel_count), jnp.float32)
    summed = jnp.stack(
        [blank if entry_value is None else entry_value for entry_value in results], axis=1
    )
    return (summed, zero_out[:, 0])


def body(
    embeddings,
    neighbours,
    valid,
    azimuth,
    polar,
    distance,
    send_low,
    send_high,
    w_zero,
    w_one_re,
    w_one_im,
    w_two_re,
    w_two_im,
    radial_weight,
    readout,
):
    atom_rows = embeddings.shape[0]
    coeffs = embeddings.shape[1]
    channel_count = embeddings.shape[2]
    degrees = math.isqrt(coeffs)
    ghost_rows = send_low.shape[0]
    slab_devices = lax.axis_size("yz")
    table_rows = slab_devices * (atom_rows + 2 * ghost_rows)
    current = embeddings
    scalar_out = None
    for layer_index in range(LAYERS):
        outgoing = current
        low_piece = outgoing[send_low]
        high_piece = outgoing[send_high]
        below_one = from_behind(high_piece, "slab", 1)
        above_one = from_behind(low_piece, "slab", -1)
        own_rows, below_rows, above_rows = (
            lax.all_gather(outgoing, "yz", axis=0, tiled=True),
            lax.all_gather(below_one, "yz", axis=0, tiled=True),
            lax.all_gather(above_one, "yz", axis=0, tiled=True),
        )
        table = jnp.concatenate([own_rows, below_rows, above_rows], axis=0)
        table = grouped_rows(table, degrees)
        summed, scalar_out = convolve(
            table[neighbours],
            degrees,
            channel_count,
            azimuth,
            distance,
            valid,
            w_zero[layer_index],
            w_one_re[layer_index],
            w_one_im[layer_index],
            w_two_re[layer_index],
            w_two_im[layer_index],
            radial_weight[layer_index],
        )
        current = (current.astype(jnp.float32) + 0.18 * summed).astype(jnp.bfloat16)
    strength = 0.125 * jnp.dot(scalar_out, readout, precision=HIGHEST)
    direction = jnp.stack(
        [jnp.sin(polar) * jnp.cos(azimuth), jnp.sin(polar) * jnp.sin(azimuth), jnp.cos(polar)],
        axis=0,
    )
    pull = direction * strength[None, :]
    own_force = pull.reshape(3, -1, NEIGHB).sum(axis=-1)
    onehot = (neighbours[:, None] == jnp.arange(table_rows, dtype=jnp.int32)[None, :]).astype(
        jnp.float32
    )
    table_force = -jnp.dot(pull, onehot, precision=HIGHEST)
    own_count = slab_devices * atom_rows
    ghost_count = slab_devices * ghost_rows
    below_force = table_force[:, own_count : own_count + ghost_count]
    above_force = table_force[:, own_count + ghost_count :]
    below_back = from_behind(below_force, "slab", -1)
    above_back = from_behind(above_force, "slab", 1)
    own_sum, high_sum, low_sum = (
        lax.psum_scatter(table_force[:, :own_count], "yz", scatter_dimension=1, tiled=True),
        lax.psum_scatter(below_back, "yz", scatter_dimension=1, tiled=True),
        lax.psum_scatter(above_back, "yz", scatter_dimension=1, tiled=True),
    )
    atom_ids = jnp.arange(atom_rows, dtype=jnp.int32)
    high_hot = (send_high[:, None] == atom_ids[None, :]).astype(jnp.float32)
    low_hot = (send_low[:, None] == atom_ids[None, :]).astype(jnp.float32)
    forces = (
        own_force
        + own_sum
        + jnp.dot(high_sum, high_hot, precision=HIGHEST)
        + jnp.dot(low_sum, low_hot, precision=HIGHEST)
    )
    return (current, forces)


def solution(mesh):
    in_specs = (
        P(("slab", "yz"), None, None),
        P(("slab", "yz")),
        P(("slab", "yz")),
        P(("slab", "yz")),
        P(("slab", "yz")),
        P(("slab", "yz")),
        P(("slab", "yz")),
        P(("slab", "yz")),
        P(),
        P(),
        P(),
        P(),
        P(),
        P(),
        P(),
    )
    out_specs = (P(("slab", "yz"), None, None), P(None, ("slab", "yz")))
    return jax.shard_map(body, mesh=mesh, in_specs=in_specs, out_specs=out_specs, check_vma=False)
```

profile of v0, /device:TPU:0, one launch (start us, length us, event | category | flops | bytes accessed | tf_op | source)
XLA Modules:
  0.0 160.3 jit_solution(2242063938275191311)
XLA Ops:
  7.2 0.7 compare_select_fusion.1
  7.9 0.7 compare_select_fusion.2
  8.6 1.7 %gather_fusion = bf16[8,25,128]{2,0,1:T(8,128)(2,1)S(1)} fusion(bf16[16,25,128]{2,0,1:T(8,128)(2,1)} %param.15, s32[1024]{0:T(1024)S(1)} %get-tuple-element.111), kind=kCustom, calls=%fused_computation | custom fusion | bytes 102432 | tf_op jit(solution)/shard_map/gather | solution.py:159
  10.4 3.0 %collective-permute-start = (bf16[8,25,128]{2,0,1:T(8,128)(2,1)S(1)}, bf16[8,25,128]{2,0,1:T(8,128)(2,1)}, u32[]{:S(2)}, u32[]{:S(2)}) collective-permute-start(bf16[8,25,128]{2,0,1:T(8,128)(2,1)S(1)} %gather_fusion), channel_id=1, source_target_pairs={{28,0},{0,4},{4,8},{8,12},{12,16},{16,20},{20,24},{24,28},{29,1},{... | collective-permute-start | bytes 153608 | tf_op jit(solution)/shard_map/ppermute | solution.py:18
  13.4 1.6 %gather_fusion.1 = bf16[8,25,128]{2,0,1:T(8,128)(2,1)S(1)} fusion(bf16[16,25,128]{2,0,1:T(8,128)(2,1)} %param.15, s32[1024]{0:T(1024)S(1)} %get-tuple-element.110), kind=kCustom, calls=%fused_computation.1 | custom fusion | bytes 102432 | tf_op jit(solution)/shard_map/gather | solution.py:158
  15.0 3.1 %collective-permute-start.1 = (bf16[8,25,128]{2,0,1:T(8,128)(2,1)S(1)}, bf16[8,25,128]{2,0,1:T(8,128)(2,1)S(1)}, u32[]{:S(2)}, u32[]{:S(2)}) collective-permute-start(bf16[8,25,128]{2,0,1:T(8,128)(2,1)S(1)} %gather_fusion.1), channel_id=1, source_target_pairs={{4,0},{8,4},{12,8},{16,12},{20,16},{24,20},{28,24},{0,28},{5,1},{9... | collective-permute-start | bytes 153608 | tf_op jit(solution)/shard_map/ppermute | solution.py:18
  18.1 6.9 %all_gather.18 = bf16[64,25,128]{2,0,1:T(8,128)(2,1)S(1)} all-gather(bf16[16,25,128]{2,0,1:T(8,128)(2,1)} %param.15), channel_id=1, replica_groups=mesh['slab'=8,'yz'=4] {'yz'}, dimensions={0}, use_global_device_ids=true | all-gather | bytes 512000 | tf_op jit(solution)/shard_map/all_gather | solution.py:163
  25.1 0.7 convert_element_type.68
  25.7 2.1 %multiply_multiply_fusion.1 = f32[512,128]{1,0:T(8,128)} fusion(f32[512]{0:T(512)S(1)} %convert_element_type.68, f32[8]{0:T(128)S(1)} %multiply_add_fusion, f32[512]{0:T(512)} %param.20, f32[2,8,128]{2,1,0:T(8,128)} %param.28), kind=kOutput, calls=%fused_computation.103 | convolution fusion | flops 6635520 | bytes 270368 | tf_op jit(solution)/shard_map/dot_general | solution.py:28
  27.8 1.4 multiply_multiply_fusion
  29.2 0.9 constant_dynamic-update-slice_fusion.2
  30.8 1.3 copy.305
  32.1 1.3 copy.314
  33.4 0.7 stack.28
  34.1 0.7 stack.29
  34.7 0.7 stack.30
  35.4 0.6 dynamic-slice
  36.8 5.9 %all_gather.19 = bf16[32,25,128]{2,0,1:T(8,128)(2,1)S(1)} all-gather(bf16[8,25,128]{2,0,1:T(8,128)(2,1)} %collective-permute-done), channel_id=1, replica_groups=mesh['slab'=8,'yz'=4] {'yz'}, dimensions={0}, use_global_device_ids=true | all-gather | bytes 256000 | tf_op jit(solution)/shard_map/all_gather | solution.py:164
  42.7 5.8 %all_gather.20 = bf16[32,25,128]{2,0,1:T(8,128)(2,1)S(1)} all-gather(bf16[8,25,128]{2,0,1:T(8,128)(2,1)S(1)} %collective-permute-done.1), channel_id=1, replica_groups=mesh['slab'=8,'yz'=4] {'yz'}, dimensions={0}, use_global_device_ids=true | all-gather | bytes 256000 | tf_op jit(solution)/shard_map/all_gather | solution.py:165
  48.9 2.6 %gather_fusion.2 = bf16[512,2432]{1,0:T(8,128)(2,1)S(1)} fusion(bf16[128,2432]{1,0:T(8,128)(2,1)S(1)} %constant_dynamic-update-slice_fusion.3, s32[1024]{0:T(1024)S(1)} %pad_clamp_fusion), kind=kCustom, calls=%fused_computation.2 | custom fusion | bytes 4982784 | tf_op jit(solution)/shard_map/gather | solution.py:170
  51.8 1.4 fusion.47
  53.1 1.3 fusion.43
  54.9 1.3 reshape.134
  56.2 1.7 %convolution_add_fusion.3 = f32[512,384]{1,0:T(8,128)S(1)} fusion(f32[512,384]{1,0:T(8,128)} %fusion.43, bf16[2,384,384]{2,1,0:T(8,128)(2,1)} %param.26, f32[512]{0:T(512)S(1)} %get-tuple-element.106, f32[512]{0:T(512)S(1)} %get-tuple-element.104, bf16[512,2432]{1,0:T(8,128)(2,1)S(1)} %gather_fusion.2), kind=kOutput, calls=%fused_computation.24 | convolution fusion | flops 152371200 | bytes 2658304 | tf_op jit(solution)/shard_map/dot_general | solution.py:105
  57.9 1.3 reshape.135
  59.2 2.6 %subtract_reduce_fusion.2 = (f32[16,3,128]{2,1,0:T(4,128)S(1)}, f32[16,3,128]{2,1,0:T(4,128)S(1)}) fusion(f32[16,32,3,128]{3,2,1,0:T(4,128)} %reshape.135, f32[16,32,3,128]{3,2,1,0:T(4,128)} %reshape.134, f32[16,32]{1,0:T(8,128)S(1)} %mul.428, f32[16,32,128]{2,1,0:T(8,128)} %bitcast.261, f32[16,32]{1,0:T(8,128)S(1)} %mul.417), kind=kLoop, calls=%fused_computation.41 | loop fusion | flops 1953792 | bytes 1888256 | tf_op jit(solution)/shard_map/reduce_sum | solution.py:112
  62.5 1.6 fusion.23
  64.1 1.5 convolution_subtract_fusion.1
  65.6 2.5 %reshape.132 = f32[16,32,4,128]{3,2,1,0:T(4,128)} reshape(f32[512,512]{1,0:T(8,128)} %convolution_subtract_fusion.1) | data formatting | bytes 2097152 | tf_op jit(solution)/shard_map/reshape | solution.py:102
  68.2 3.0 %convolution_add_fusion.1 = f32[512,512]{1,0:T(8,128)} fusion(f32[512,512]{1,0:T(8,128)} %fusion.23, bf16[2,512,512]{2,1,0:T(8,128)(2,1)} %param.24, f32[512]{0:T(512)S(1)} %get-tuple-element.105, f32[512]{0:T(512)S(1)} %get-tuple-element.107, bf16[512,2432]{1,0:T(8,128)(2,1)S(1)} %gather_fusion.2), kind=kOutput, calls=%fused_computation.10 | convolution fusion | flops 270270464 | bytes 3674112 | tf_op jit(solution)/shard_map/dot_general | solution.py:105
  71.1 2.5 %reshape.133 = f32[16,32,4,128]{3,2,1,0:T(4,128)} reshape(f32[512,512]{1,0:T(8,128)} %convolution_add_fusion.1) | data formatting | bytes 2097152 | tf_op jit(solution)/shard_map/reshape | solution.py:106
  73.7 2.5 %subtract_reduce_fusion.3 = (f32[16,4,128]{2,1,0:T(4,128)S(1)}, f32[16,4,128]{2,1,0:T(4,128)S(1)}) fusion(f32[16,32,4,128]{3,2,1,0:T(4,128)} %reshape.133, f32[16,32,4,128]{3,2,1,0:T(4,128)} %reshape.132, f32[16,32]{1,0:T(8,128)S(1)} %mul.410, f32[16,32,128]{2,1,0:T(8,128)S(1)} %bitcast.262, f32[16,32]{1,0:T(8,128)S(1)} %mul.398), kind=kLoop, calls=%fused_computation.43 | loop fusion | flops 2605056 | bytes 2428928 | tf_op jit(solution)/shard_map/reduce_sum | solution.py:112
  76.3 0.8 bitcast_reduce_fusion.1
  78.4 0.7 gather_fusion.3
  79.0 6.7 %all_gather.21 = bf16[64,25,128]{2,0,1:T(8,128)(2,1)S(1)} all-gather(bf16[16,25,128]{2,0,1:T(8,128)(2,1)S(1)} %copy.311), channel_id=1, replica_groups=mesh['slab'=8,'yz'=4] {'yz'}, dimensions={0}, use_global_device_ids=true | all-gather | bytes 512000 | tf_op jit(solution)/shard_map/all_gather | solution.py:163
  85.7 0.7 gather_fusion.4
  86.4 4.8 %collective-permute-start.3 = (bf16[8,25,128]{2,1,0:T(8,128)(2,1)S(1)}, bf16[8,25,128]{2,1,0:T(8,128)(2,1)S(1)}, u32[]{:S(2)}, u32[]{:S(2)}) collective-permute-start(bf16[8,25,128]{2,1,0:T(8,128)(2,1)S(1)} %gather_fusion.4), channel_id=1, source_target_pairs={{4,0},{8,4},{12,8},{16,12},{20,16},{24,20},{28,24},{0,28},{5,1},{9... | collective-permute-start | bytes 153608 | tf_op jit(solution)/shard_map/ppermute | solution.py:18
  91.2 1.5 collective-permute-done.2
  92.8 5.7 %all_gather.22 = bf16[32,25,128]{2,0,1:T(8,128)(2,1)S(1)} all-gather(bf16[8,25,128]{2,0,1:T(8,128)(2,1)S(1)} %copy.312), channel_id=1, replica_groups=mesh['slab'=8,'yz'=4] {'yz'}, dimensions={0}, use_global_device_ids=true | all-gather | bytes 256000 | tf_op jit(solution)/shard_map/all_gather | solution.py:164
  98.5 5.9 %all_gather.23 = bf16[32,25,128]{2,0,1:T(8,128)(2,1)S(1)} all-gather(bf16[8,25,128]{2,0,1:T(8,128)(2,1)S(1)} %copy.313), channel_id=1, replica_groups=mesh['slab'=8,'yz'=4] {'yz'}, dimensions={0}, use_global_device_ids=true | all-gather | bytes 256000 | tf_op jit(solution)/shard_map/all_gather | solution.py:165
  104.8 2.6 %gather_fusion.5 = bf16[512,2432]{1,0:T(8,128)(2,1)S(1)} fusion(bf16[128,2432]{1,0:T(8,128)(2,1)S(1)} %constant_dynamic-update-slice_fusion.25, s32[1024]{0:T(1024)S(1)} %copy-done.41), kind=kCustom, calls=%fused_computation.5 | custom fusion | bytes 4982784 | tf_op jit(solution)/shard_map/gather | solution.py:170
  107.6 1.5 fusion.41
  109.2 1.3 fusion.37
  110.5 1.5 fusion.21
  112.0 1.6 fusion.17
  113.6 1.4 bitcast_reduce_fusion
  115.4 0.7 mul.467
  116.3 0.7 fusion.108
  117.0 2.0 %collective-permute-start.5 = (f32[3,32]{1,0:T(4,128)}, f32[3,32]{1,0:T(4,128)}, u32[]{:S(2)}, u32[]{:S(2)}) collective-permute-start(f32[3,32]{1,0:T(4,128)} %get-tuple-element.99), channel_id=1, source_target_pairs={{28,0},{0,4},{4,8},{8,12},{12,16},{16,20},{20,24},{24,28},{29,1},{... | collective-permute-start | bytes 1160 | tf_op jit(solution)/shard_map/ppermute | solution.py:18
  119.1 0.7 copy.321
  119.8 2.3 %convolution_subtract_fusion.2 = f32[512,384]{1,0:T(8,128)} fusion(f32[512,384]{1,0:T(8,128)S(1)} %fusion.41, bf16[2,384,384]{2,1,0:T(8,128)(2,1)} %param.27, f32[512]{0:T(512)S(1)} %get-tuple-element.106, f32[512]{0:T(512)S(1)} %get-tuple-element.104, bf16[512,2432]{1,0:T(8,128)(2,1)S(1)} %gather_fusion.5), kind=kOutput, calls=%fused_computation.23 | convolution fusion | flops 152371200 | bytes 2658304 | tf_op jit(solution)/shard_map/dot_general | solution.py:101
  122.1 1.4 reshape.139
  123.6 2.6 %convolution_add_fusion.2 = f32[512,384]{1,0:T(8,128)} fusion(f32[512,384]{1,0:T(8,128)} %fusion.37, bf16[2,384,384]{2,1,0:T(8,128)(2,1)} %param.26, f32[512]{0:T(512)} %copy-done.21, f32[512]{0:T(512)S(1)} %get-tuple-element.104, bf16[512,2432]{1,0:T(8,128)(2,1)S(1)} %gather_fusion.5), kind=kOutput, calls=%fused_computation.22 | convolution fusion | flops 152371200 | bytes 2658304 | tf_op jit(solution)/shard_map/dot_general | solution.py:105
  126.2 2.3 %reshape.140 = f32[16,32,3,128]{3,2,1,0:T(4,128)} reshape(f32[512,384]{1,0:T(8,128)} %convolution_add_fusion.2) | data formatting | bytes 1572864 | tf_op jit(solution)/shard_map/reshape | solution.py:106
  128.5 3.3 %subtract_reduce_fusion = (f32[16,3,128]{2,1,0:T(4,128)S(1)}, f32[16,3,128]{2,1,0:T(4,128)S(1)}) fusion(f32[16,32,3,128]{3,2,1,0:T(4,128)} %reshape.140, f32[16,32,3,128]{3,2,1,0:T(4,128)S(1)} %reshape.139, f32[16,32,128]{2,1,0:T(8,128)} %bitcast.259, f32[16,32]{1,0:T(8,128)} %copy-done.29, f32[16,32]{1,0:T(8,128)} %copy-done.28), kind=kLoop, calls=%fused_computation.37 | loop fusion | flops 1953792 | bytes 1888256 | tf_op jit(solution)/shard_map/reduce_sum | solution.py:112
  133.0 1.6 convolution_subtract_fusion
  134.6 1.6 reshape.137
  136.1 3.0 %convolution_add_fusion = f32[512,512]{1,0:T(8,128)} fusion(f32[512,512]{1,0:T(8,128)} %fusion.17, bf16[2,512,512]{2,1,0:T(8,128)(2,1)} %param.24, f32[512]{0:T(512)S(1)} %copy-done.23, f32[512]{0:T(512)} %copy-done.24, bf16[512,2432]{1,0:T(8,128)(2,1)S(1)} %gather_fusion.5), kind=kOutput, calls=%fused_computation.8 | convolution fusion | flops 270270464 | bytes 3674112 | tf_op jit(solution)/shard_map/dot_general | solution.py:105
  139.2 1.7 %reshape.138 = f32[16,32,4,128]{3,2,1,0:T(4,128)S(1)} reshape(f32[512,512]{1,0:T(8,128)} %convolution_add_fusion) | data formatting | bytes 2097152 | tf_op jit(solution)/shard_map/reshape | solution.py:106
  140.9 2.8 %subtract_reduce_fusion.1 = (f32[16,4,128]{2,1,0:T(4,128)S(1)}, f32[16,4,128]{2,1,0:T(4,128)S(1)}) fusion(f32[16,32,4,128]{3,2,1,0:T(4,128)S(1)} %reshape.138, f32[16,32,4,128]{3,2,1,0:T(4,128)S(1)} %reshape.137, f32[16,32,128]{2,1,0:T(8,128)} %bitcast.260, f32[16,32]{1,0:T(8,128)} %copy-done.27, f32[16,32]{1,0:T(8,128)} %copy-done.26), kind=kLoop, calls=%fused_computation.39 | loop fusion | flops 2605056 | bytes 2428928 | tf_op jit(solution)/shard_map/reduce_sum | solution.py:112
  144.6 0.7 copy.320
  145.3 6.5 %all-reduce.2 = (f32[3,32]{1,0:T(4,128)S(1)}, f32[3,32]{1,0:T(4,128)S(1)}) all-reduce(f32[3,32]{1,0:T(4,128)} %collective-permute-done.5, f32[3,32]{1,0:T(4,128)} %collective-permute-done.4), channel_id=4, replica_groups=mesh['slab'=8,'yz'=4] {'yz'}, use_global_device_ids=true, to_apply=%region_13.14.clone | all-reduce | flops 192 | bytes 1536
  151.9 0.8 copy.322
  152.7 0.8 fusion
  (211 shorter events, 7.0 us)
Async XLA Ops:
  7.2 107.9 %copy-start = (f32[128]{0:T(128)S(1)}, f32[128]{0:T(128)}, u32[]{:S(2)}) copy-start(f32[128]{0:T(128)} %param.29) | copy-start | bytes 1540
  7.2 20.6 %copy-start.55 = (f32[512]{0:T(512)S(1)}, f32[512]{0:T(512)}, u32[]{:S(2)}) copy-start(f32[512]{0:T(512)} %param.20) | copy-start | bytes 6148
  7.2 20.6 %copy-start.54 = (f32[2,8,128]{2,1,0:T(8,128)S(1)}, f32[2,8,128]{2,1,0:T(8,128)}, u32[]{:S(2)}) copy-start(f32[2,8,128]{2,1,0:T(8,128)} %param.28) | copy-start | bytes 24580
  7.2 144.7 %reduce-scatter.6.cloned.1.call-start = ((), (), s32[]{:S(2)}) async-start(), calls=%async_computation.1 | async-start | bytes 40960
  8.6 4.8 %copy-start.49 = (s32[1024]{0:T(1024)}, s32[1024]{0:T(1024)S(1)}, u32[]{:S(2)}) copy-start(s32[1024]{0:T(1024)S(1)} %get-tuple-element.111) | copy-start | bytes 12292
  8.6 21.5 %copy-start.48 = (s32[1024]{0:T(1024)}, s32[1024]{0:T(1024)S(1)}, u32[]{:S(2)}) copy-start(s32[1024]{0:T(1024)S(1)} %get-tuple-element.110) | copy-start | bytes 12292
  8.6 21.5 %copy-start.52 = (s32[512]{0:T(512)S(1)}, s32[512]{0:T(512)}, u32[]{:S(2)}) copy-start(s32[512]{0:T(512)} %param.16) | copy-start | bytes 6148
  8.6 21.5 %copy-start.50 = (f32[512]{0:T(512)S(1)}, f32[512]{0:T(512)}, u32[]{:S(2)}) copy-start(f32[512]{0:T(512)} %param.18) | copy-start | bytes 6148
  8.6 21.5 %copy-start.8 = (bf16[2,640,640]{2,1,0:T(8,128)(2,1)S(1)}, bf16[2,640,640]{2,1,0:T(8,128)(2,1)}, u32[]{:S(2)}) copy-start(bf16[2,640,640]{2,1,0:T(8,128)(2,1)} %param.23) | copy-start | bytes 4915204
  10.4 26.4 %collective-permute-start = (bf16[8,25,128]{2,0,1:T(8,128)(2,1)S(1)}, bf16[8,25,128]{2,0,1:T(8,128)(2,1)}, u32[]{:S(2)}, u32[]{:S(2)}) collective-permute-start(bf16[8,25,128]{2,0,1:T(8,128)(2,1)S(1)} %gather_fusion), channel_id=1, source_target_pairs={{28,0},{0,4},{4,8},{8,12},{12,16},{16,20},{20,24},{24,28},{29,1},{... | collective-permute-start | bytes 153608 | tf_op jit(solution)/shard_map/ppermute | solution.py:18
  15.0 27.7 %collective-permute-start.1 = (bf16[8,25,128]{2,0,1:T(8,128)(2,1)S(1)}, bf16[8,25,128]{2,0,1:T(8,128)(2,1)S(1)}, u32[]{:S(2)}, u32[]{:S(2)}) collective-permute-start(bf16[8,25,128]{2,0,1:T(8,128)(2,1)S(1)} %gather_fusion.1), channel_id=1, source_target_pairs={{4,0},{8,4},{12,8},{16,12},{20,16},{24,20},{28,24},{0,28},{5,1},{9... | collective-permute-start | bytes 153608 | tf_op jit(solution)/shard_map/ppermute | solution.py:18
  27.8 2.5 %copy-start.51 = (f32[512]{0:T(512)S(1)}, f32[512]{0:T(512)}, u32[]{:S(2)}) copy-start(f32[512]{0:T(512)} %param.19) | copy-start | bytes 6148
  30.2 81.8 %copy-start.22 = (f32[512]{0:T(512)}, f32[512]{0:T(512)S(1)}, u32[]{:S(2)}) copy-start(f32[512]{0:T(512)S(1)} %get-tuple-element.105) | copy-start | bytes 6148
  30.2 81.8 %copy-start.24 = (f32[512]{0:T(512)}, f32[512]{0:T(512)S(1)}, u32[]{:S(2)}) copy-start(f32[512]{0:T(512)S(1)} %get-tuple-element.107) | copy-start | bytes 6148
  30.2 89.6 %copy-start.21 = (f32[512]{0:T(512)}, f32[512]{0:T(512)S(1)}, u32[]{:S(2)}) copy-start(f32[512]{0:T(512)S(1)} %get-tuple-element.106) | copy-start | bytes 6148
  30.4 5.1 %copy-start.58 = (u32[32]{0:T(128)S(1)}, u32[32]{0:T(128)}, u32[]{:S(2)}) copy-start(u32[32]{0:T(128)} %constant.31) | copy-start | bytes 388
  30.4 12.2 %copy-start.9 = (bf16[128,25,128]{2,0,1:T(8,128)(2,1)S(1)}, bf16[128,25,128]{2,0,1:T(8,128)(2,1)}, u32[]{:S(2)}) copy-start(bf16[128,25,128]{2,0,1:T(8,128)(2,1)} %constant_dynamic-update-slice_fusion.2) | copy-start | bytes 2457604
  30.4 18.2 %copy-start.42 = (f32[512]{0:T(512)}, f32[512]{0:T(512)S(1)}, u32[]{:S(2)}) copy-start(f32[512]{0:T(512)S(1)} %get-tuple-element.103) | copy-start | bytes 6148
  30.4 18.2 %copy-start.44 = (f32[512]{0:T(512)}, f32[512]{0:T(512)S(1)}, u32[]{:S(2)}) copy-start(f32[512]{0:T(512)S(1)} %get-tuple-element.100) | copy-start | bytes 6148
  30.5 18.2 %copy-start.46 = (f32[512]{0:T(512)}, f32[512]{0:T(512)S(1)}, u32[]{:S(2)}) copy-start(f32[512]{0:T(512)S(1)} %get-tuple-element.101) | copy-start | bytes 6148
  30.5 18.4 %copy-start.40 = (s32[1024]{0:T(1024)}, s32[1024]{0:T(1024)S(1)}, u32[]{:S(2)}) copy-start(s32[1024]{0:T(1024)S(1)} %pad_clamp_fusion) | copy-start | bytes 12292
  30.6 43.1 %copy-start.26 = (f32[16,32]{1,0:T(8,128)}, f32[16,32]{1,0:T(8,128)S(1)}, u32[]{:S(2)}) copy-start(f32[16,32]{1,0:T(8,128)S(1)} %mul.398) | copy-start | bytes 6148
  30.6 43.0 %copy-start.27 = (f32[16,32]{1,0:T(8,128)}, f32[16,32]{1,0:T(8,128)S(1)}, u32[]{:S(2)}) copy-start(f32[16,32]{1,0:T(8,128)S(1)} %mul.410) | copy-start | bytes 6148
  30.7 28.5 %copy-start.28 = (f32[16,32]{1,0:T(8,128)}, f32[16,32]{1,0:T(8,128)S(1)}, u32[]{:S(2)}) copy-start(f32[16,32]{1,0:T(8,128)S(1)} %mul.417) | copy-start | bytes 6148
  30.8 28.4 %copy-start.29 = (f32[16,32]{1,0:T(8,128)}, f32[16,32]{1,0:T(8,128)S(1)}, u32[]{:S(2)}) copy-start(f32[16,32]{1,0:T(8,128)S(1)} %mul.428) | copy-start | bytes 6148
  59.2 2.7 %copy-start.15 = (bf16[2,512,512]{2,1,0:T(8,128)(2,1)S(1)}, bf16[2,512,512]{2,1,0:T(8,128)(2,1)}, u32[]{:S(2)}) copy-start(bf16[2,512,512]{2,1,0:T(8,128)(2,1)} %param.24) | copy-start | bytes 3145732
  59.2 3.3 %copy-start.12 = (bf16[2,512,512]{2,1,0:T(8,128)(2,1)S(1)}, bf16[2,512,512]{2,1,0:T(8,128)(2,1)}, u32[]{:S(2)}) copy-start(bf16[2,512,512]{2,1,0:T(8,128)(2,1)} %param.25) | copy-start | bytes 3145732
  68.2 5.5 %copy-start.10 = (f32[512,128]{1,0:T(8,128)S(1)}, f32[512,128]{1,0:T(8,128)}, u32[]{:S(2)}) copy-start(f32[512,128]{1,0:T(8,128)} %multiply_multiply_fusion.1) | copy-start | bytes 786436
  73.7 2.6 %copy-start.17 = (bf16[640,640]{1,0:T(8,128)(2,1)S(1)}, bf16[640,640]{1,0:T(8,128)(2,1)}, u32[]{:S(2)}) copy-start(bf16[640,640]{1,0:T(8,128)(2,1)} %copy.305) | copy-start | bytes 2457604
  76.2 2.0 %copy-start.1 = (bf16[16,25,128]{2,0,1:T(8,128)(2,1)S(1)}, bf16[16,25,128]{2,0,1:T(8,128)(2,1)}, u32[]{:S(2)}) copy-start(bf16[16,25,128]{2,0,1:T(8,128)(2,1)} %param.15) | copy-start | bytes 307204
  78.2 26.5 %copy-start.41 = (s32[1024]{0:T(1024)S(1)}, s32[1024]{0:T(1024)}, u32[]{:S(2)}) copy-start(s32[1024]{0:T(1024)} %copy-done.40) | copy-start | bytes 12292
  78.3 26.4 %copy-start.6 = (bf16[16,25,128]{2,1,0:T(8,128)(2,1)}, bf16[16,25,128]{2,1,0:T(8,128)(2,1)S(1)}, u32[]{:S(2)}) copy-start(bf16[16,25,128]{2,1,0:T(8,128)(2,1)S(1)} %add_convert_fusion.1) | copy-start | bytes 307204
  85.7 7.0 %collective-permute-start.2 = (bf16[8,25,128]{2,1,0:T(8,128)(2,1)S(1)}, bf16[8,25,128]{2,1,0:T(8,128)(2,1)S(1)}, u32[]{:S(2)}, u32[]{:S(2)}) collective-permute-start(bf16[8,25,128]{2,1,0:T(8,128)(2,1)S(1)} %gather_fusion.3), channel_id=1, source_target_pairs={{28,0},{0,4},{4,8},{8,12},{12,16},{16,20},{20,24},{24,28},{29,1},{... | collective-permute-start | bytes 153608 | tf_op jit(solution)/shard_map/ppermute | solution.py:18
  86.4 12.0 %collective-permute-start.3 = (bf16[8,25,128]{2,1,0:T(8,128)(2,1)S(1)}, bf16[8,25,128]{2,1,0:T(8,128)(2,1)S(1)}, u32[]{:S(2)}, u32[]{:S(2)}) collective-permute-start(bf16[8,25,128]{2,1,0:T(8,128)(2,1)S(1)} %gather_fusion.4), channel_id=1, source_target_pairs={{4,0},{8,4},{12,8},{16,12},{20,16},{24,20},{28,24},{0,28},{5,1},{9... | collective-permute-start | bytes 153608 | tf_op jit(solution)/shard_map/ppermute | solution.py:18
  107.4 1.8 %copy-start.4 = (bf16[2,384,384]{2,1,0:T(8,128)(2,1)S(1)}, bf16[2,384,384]{2,1,0:T(8,128)(2,1)}, u32[]{:S(2)}) copy-start(bf16[2,384,384]{2,1,0:T(8,128)(2,1)} %param.27) | copy-start | bytes 1769476
  107.4 3.1 %copy-start.16 = (bf16[2,512,512]{2,1,0:T(8,128)(2,1)S(1)}, bf16[2,512,512]{2,1,0:T(8,128)(2,1)}, u32[]{:S(2)}) copy-start(bf16[2,512,512]{2,1,0:T(8,128)(2,1)} %param.24) | copy-start | bytes 3145732
  109.1 2.9 %copy-start.13 = (bf16[2,512,512]{2,1,0:T(8,128)(2,1)S(1)}, bf16[2,512,512]{2,1,0:T(8,128)(2,1)}, u32[]{:S(2)}) copy-start(bf16[2,512,512]{2,1,0:T(8,128)(2,1)} %param.25) | copy-start | bytes 3145732
  110.4 3.1 %copy-start.2 = (bf16[640,640]{1,0:T(8,128)(2,1)S(1)}, bf16[640,640]{1,0:T(8,128)(2,1)}, u32[]{:S(2)}) copy-start(bf16[640,640]{1,0:T(8,128)(2,1)} %copy.314) | copy-start | bytes 2457604
  110.5 3.1 %copy-start.5 = (f32[512,128]{1,0:T(8,128)S(1)}, f32[512,128]{1,0:T(8,128)}, u32[]{:S(2)}) copy-start(f32[512,128]{1,0:T(8,128)} %multiply_multiply_fusion) | copy-start | bytes 786436
  112.0 4.0 %copy-start.43 = (f32[512]{0:T(512)S(1)}, f32[512]{0:T(512)}, u32[]{:S(2)}) copy-start(f32[512]{0:T(512)} %copy-done.42) | copy-start | bytes 6148
  112.0 4.0 %copy-start.45 = (f32[512]{0:T(512)S(1)}, f32[512]{0:T(512)}, u32[]{:S(2)}) copy-start(f32[512]{0:T(512)} %copy-done.44) | copy-start | bytes 6148
  112.0 4.0 %copy-start.47 = (f32[512]{0:T(512)S(1)}, f32[512]{0:T(512)}, u32[]{:S(2)}) copy-start(f32[512]{0:T(512)} %copy-done.46) | copy-start | bytes 6148
  112.0 4.0 %copy-start.53 = (s32[512]{0:T(512)S(1)}, s32[512]{0:T(512)}, u32[]{:S(2)}) copy-start(s32[512]{0:T(512)} %param.16) | copy-start | bytes 6148
  117.0 28.2 %collective-permute-start.4 = (f32[3,32]{1,0:T(4,128)}, f32[3,32]{1,0:T(4,128)}, u32[]{:S(2)}, u32[]{:S(2)}) collective-permute-start(f32[3,32]{1,0:T(4,128)} %get-tuple-element.98), channel_id=1, source_target_pairs={{4,0},{8,4},{12,8},{16,12},{20,16},{24,20},{28,24},{0,28},{5,1},{9... | collective-permute-start | bytes 1160 | tf_op jit(solution)/shard_map/ppermute | solution.py:18
  117.0 28.2 %collective-permute-start.5 = (f32[3,32]{1,0:T(4,128)}, f32[3,32]{1,0:T(4,128)}, u32[]{:S(2)}, u32[]{:S(2)}) collective-permute-start(f32[3,32]{1,0:T(4,128)} %get-tuple-element.99), channel_id=1, source_target_pairs={{28,0},{0,4},{4,8},{8,12},{12,16},{16,20},{20,24},{24,28},{29,1},{... | collective-permute-start | bytes 1160 | tf_op jit(solution)/shard_map/ppermute | solution.py:18
  126.2 6.8 %copy-start.23 = (f32[512]{0:T(512)S(1)}, f32[512]{0:T(512)}, u32[]{:S(2)}) copy-start(f32[512]{0:T(512)} %copy-done.22) | copy-start | bytes 6148
  128.5 4.5 %copy-start.11 = (f32[512,512]{1,0:T(8,128)S(1)}, f32[512,512]{1,0:T(8,128)}, u32[]{:S(2)}) copy-start(f32[512,512]{1,0:T(8,128)} %fusion.21) | copy-start | bytes 3145732
  128.5 4.5 %copy-start.14 = (bf16[2,512,512]{2,1,0:T(8,128)(2,1)S(1)}, bf16[2,512,512]{2,1,0:T(8,128)(2,1)}, u32[]{:S(2)}) copy-start(bf16[2,512,512]{2,1,0:T(8,128)(2,1)} %param.25) | copy-start | bytes 3145732
  128.5 4.5 %copy-start.25 = (f32[512]{0:T(512)S(1)}, f32[512]{0:T(512)}, u32[]{:S(2)}) copy-start(f32[512]{0:T(512)} %copy-done.24) | copy-start | bytes 6148
  139.1 4.7 %copy-start.20 = (f32[16,5,128]{2,0,1:T(8,128)S(1)}, f32[16,5,128]{2,0,1:T(8,128)}, u32[]{:S(2)}) copy-start(f32[16,5,128]{2,0,1:T(8,128)} %get-tuple-element.108) | copy-start | bytes 122884
  139.1 4.8 %copy-start.19 = (f32[16,2,128]{2,1,0:T(2,128)S(1)}, f32[16,2,128]{2,1,0:T(2,128)}, u32[]{:S(2)}) copy-start(f32[16,2,128]{2,1,0:T(2,128)} %copy-done.18) | copy-start | bytes 49156
  139.1 4.8 %copy-start.30 = (f32[16,1,128]{2,1,0:T(1,128)S(1)}, f32[16,1,128]{2,1,0:T(1,128)}, u32[]{:S(2)}) copy-start(f32[16,1,128]{2,1,0:T(1,128)} %get-tuple-element.70) | copy-start | bytes 24580
  139.1 4.8 %copy-start.31 = (f32[16,1,128]{2,1,0:T(1,128)S(1)}, f32[16,1,128]{2,1,0:T(1,128)}, u32[]{:S(2)}) copy-start(f32[16,1,128]{2,1,0:T(1,128)} %get-tuple-element.71) | copy-start | bytes 24580
  139.1 4.8 %copy-start.32 = (f32[16,1,128]{2,1,0:T(1,128)S(1)}, f32[16,1,128]{2,1,0:T(1,128)}, u32[]{:S(2)}) copy-start(f32[16,1,128]{2,1,0:T(1,128)} %get-tuple-element.72) | copy-start | bytes 24580
  139.1 4.8 %copy-start.33 = (f32[16,1,128]{2,1,0:T(1,128)S(1)}, f32[16,1,128]{2,1,0:T(1,128)}, u32[]{:S(2)}) copy-start(f32[16,1,128]{2,1,0:T(1,128)} %get-tuple-element.81) | copy-start | bytes 24580
  139.1 4.8 %copy-start.34 = (f32[16,1,128]{2,1,0:T(1,128)S(1)}, f32[16,1,128]{2,1,0:T(1,128)}, u32[]{:S(2)}) copy-start(f32[16,1,128]{2,1,0:T(1,128)} %get-tuple-element.82) | copy-start | bytes 24580
  139.1 4.8 %copy-start.35 = (f32[16,1,128]{2,1,0:T(1,128)S(1)}, f32[16,1,128]{2,1,0:T(1,128)}, u32[]{:S(2)}) copy-start(f32[16,1,128]{2,1,0:T(1,128)} %get-tuple-element.83) | copy-start | bytes 24580
  139.1 5.2 %copy-start.7 = (bf16[16,25,128]{2,1,0:T(8,128)(2,1)S(1)}, bf16[16,25,128]{2,1,0:T(8,128)(2,1)}, u32[]{:S(2)}) copy-start(bf16[16,25,128]{2,1,0:T(8,128)(2,1)} %copy-done.6) | copy-start | bytes 307204
  139.1 5.3 %copy-start.36 = (f32[1,16,32]{2,1,0:T(8,128)S(1)}, f32[1,16,32]{2,1,0:T(8,128)}, u32[]{:S(2)}) copy-start(f32[1,16,32]{2,1,0:T(8,128)} %stack.28) | copy-start | bytes 6148
  139.1 5.3 %copy-start.37 = (f32[1,16,32]{2,1,0:T(8,128)S(1)}, f32[1,16,32]{2,1,0:T(8,128)}, u32[]{:S(2)}) copy-start(f32[1,16,32]{2,1,0:T(8,128)} %stack.29) | copy-start | bytes 6148
  139.2 5.3 %copy-start.38 = (f32[1,16,32]{2,1,0:T(8,128)S(1)}, f32[1,16,32]{2,1,0:T(8,128)}, u32[]{:S(2)}) copy-start(f32[1,16,32]{2,1,0:T(8,128)} %stack.30) | copy-start | bytes 6148
  139.2 5.3 %copy-start.39 = (f32[16,32]{1,0:T(8,128)S(1)}, f32[16,32]{1,0:T(8,128)}, u32[]{:S(2)}) copy-start(f32[16,32]{1,0:T(8,128)} %mul.467) | copy-start | bytes 6148
  140.9 10.8 %copy-start.56 = (s32[8]{0:T(128)S(1)}, s32[8]{0:T(128)}, u32[]{:S(2)}) copy-start(s32[8]{0:T(128)} %param.21) | copy-start | bytes 100
  140.9 11.8 %copy-start.57 = (s32[8]{0:T(128)S(1)}, s32[8]{0:T(128)}, u32[]{:S(2)}) copy-start(s32[8]{0:T(128)} %param.22) | copy-start | bytes 100
  (2 other events, 2.2 us)
Sparse Core Ops, SparseCore 0:
  119.9 18.5 reduce-scatter.5
where the time goes:
time: 161 us; the launch traced here: 160 us
  blocking collectives  43.3 us (27%)
  local copies, waits for them, and re-layouts  38.6 us (24%)
  matrix products  34.1 us (21%)
  between operations  15.8 us (10%)
  other arithmetic  14 us (9%)
  starting transfers between devices  13 us (8%)
    all_gather x2, blocking collectives, body(): lax.all_gather(outgoing, 'yz', axis=0, tiled=True)  13.6 us
    ppermute x6, starting transfers between devices, from_behind(): return lax.ppermute(block, axis, route)  12.9 us
    all_gather x2, blocking collectives, body(): lax.all_gather(above_one, 'yz', axis=0, tiled=True)  11.7 us
    all_gather x2, blocking collectives, body(): lax.all_gather(below_one, 'yz', axis=0, tiled=True)  11.5 us
    reduce_sum x4, other arithmetic, convolve(): back_plus = (cos_rows * out_plus - sin_rows * out_minus).reshape(atom_cou...  11.3 us
    dot_general x4, matrix products, convolve(): jnp.dot(turned_minus, real_part, preferred_element_type=jnp.float32)  10.3 us
    reshape x4, local copies, waits for them, and re-layouts, convolve(): out_minus = (jnp.dot(turned_plus, imag_part, preferred_element_type=jnp.f...  7.79 us
    reshape x4, local copies, waits for them, and re-layouts, convolve(): out_plus = (jnp.dot(turned_plus, real_part, preferred_element_type=jnp.fl...  6.82 us
  transfers between devices with their start and end apart: 7, of which 1 were waited for; matrix products, arithmetic and copies ran while one was open for 24% of the time, Pallas kernels for 0%

commit v1 on v0

v1 whole, which is shorter than its diff:
```python
import functools
import math

import jax
import jax.numpy as jnp
from jax import lax
from jax.experimental import pallas as pl
from jax.experimental.pallas import tpu as pltpu
from jax.sharding import PartitionSpec as P

LAYERS = 2
MESH = pl.DeviceIdType.MESH
HIGHEST = lax.Precision.HIGHEST
F32 = jnp.float32
BF16 = jnp.bfloat16


def slot_index(degree, order):
    return degree * degree + degree + order


def slot_groups(degrees):
    groups = [[slot_index(degree, 0) for degree in range(degrees)]]
    for order in (1, 2):
        groups.append(
            [slot_index(degree, order) for degree in range(order, degrees)]
            + [slot_index(degree, -order) for degree in range(order, degrees)]
        )
    return groups


def nt_dot(left, right, precision=None):
    return lax.dot_general(
        left, right, (((1,), (1,)), ((), ())), precision=precision, preferred_element_type=F32
    )


def kernel(
    n_slab,
    n_yz,
    atoms,
    coeffs,
    stride,
    channels,
    ghosts,
    neighb,
    groups,
    emb,
    nbr,
    val,
    azi,
    pol,
    dist,
    send_low,
    send_high,
    w_hbm0,
    w_hbm1,
    w_hbm2,
    w_hbm3,
    w_hbm4,
    radial_weight,
    readout,
    out_e,
    out_f,
    wv0,
    wv1,
    wv2,
    wv3,
    wv4,
    unpacked,
    natural,
    radp,
    picks,
    scatter,
    direction,
    f_send,
    f_recv,
    *rest,
):
    n_groups = len(groups)
    own_bufs = [rest[layer * n_groups : (layer + 1) * n_groups] for layer in range(LAYERS)]
    rest = rest[LAYERS * n_groups :]
    ghost_bufs = [rest[layer * n_groups : (layer + 1) * n_groups] for layer in range(LAYERS)]
    rest = rest[LAYERS * n_groups :]
    lend_bufs = [rest[layer * n_groups : (layer + 1) * n_groups] for layer in range(LAYERS)]
    rest = rest[LAYERS * n_groups :]
    weight_sem, send_sem, recv_sem = rest

    edges = atoms * neighb
    own_rows = n_yz * atoms
    ghost_rows = n_yz * ghosts
    table_rows = own_rows + 2 * ghost_rows
    half = n_yz // 2

    slab = lax.axis_index("slab")
    q = lax.axis_index("yz")
    above = lax.rem(slab + 1, n_slab)
    below = lax.rem(slab + n_slab - 1, n_slab)
    core = lax.rem(q, 2)
    row = q // 2
    partner = q + 1 - 2 * core

    def to_peer(j):
        return lax.rem(row + j, half) * 2 + core

    def from_peer(j):
        return lax.rem(row + half - j, half) * 2 + core

    def partner_of(index):
        return index + 1 - 2 * lax.rem(index, 2)

    weight_pairs = ((w_hbm0, wv0), (w_hbm1, wv1), (w_hbm2, wv2), (w_hbm3, wv3), (w_hbm4, wv4))
    weight_copies = [
        [
            pltpu.make_async_copy(
                source.at[layer], target.at[layer], weight_sem.at[layer * 5 + number]
            )
            for number, (source, target) in enumerate(weight_pairs)
        ]
        for layer in range(LAYERS)
    ]
    for layer in range(LAYERS):
        for copy in weight_copies[layer]:
            copy.start()

    barrier = pltpu.get_barrier_semaphore()
    peers = [(slab, lax.rem(q + j, n_yz)) for j in range(1, n_yz)]
    peers += [(above, lax.rem(q + j, n_yz)) for j in range(n_yz)]
    peers += [(below, lax.rem(q + j, n_yz)) for j in range(n_yz)]
    for peer in peers:
        pl.semaphore_signal(barrier, inc=1, device_id=peer, device_id_type=MESH)

    lend_row = lax.broadcasted_iota(jnp.int32, (2 * ghosts, atoms), 0)
    lend_col = lax.broadcasted_iota(jnp.int32, (2 * ghosts, atoms), 1)
    wanted = jnp.zeros((2 * ghosts, atoms), jnp.int32)
    for g in range(ghosts):
        wanted = jnp.where(lend_row == g, send_high[g], wanted)
        wanted = jnp.where(lend_row == ghosts + g, send_low[g], wanted)
    lend = (wanted == lend_col).astype(F32).astype(BF16)

    def lend_rows(layer, number):
        rows = jnp.dot(lend, own_bufs[layer][number][q], preferred_element_type=F32)
        lend_bufs[layer][number][0] = rows[:ghosts].astype(BF16)
        lend_bufs[layer][number][1] = rows[ghosts:].astype(BF16)

    for atom in range(atoms):
        unpacked[stride * atom : stride * atom + coeffs, :] = emb[atom].astype(F32)
    for number, group in enumerate(groups):
        for place, slot in enumerate(group):
            own_bufs[0][number][q, :, place * channels : (place + 1) * channels] = unpacked[
                pl.ds(slot, atoms, stride=stride), :
            ].astype(BF16)
        lend_rows(0, number)

    pl.semaphore_wait(barrier, len(peers))

    sends = []
    count = [0]

    def send(source, target, device):
        k = count[0]
        count[0] += 1
        copy = pltpu.make_async_remote_copy(
            src_ref=source,
            dst_ref=target,
            send_sem=send_sem.at[k],
            recv_sem=recv_sem.at[k],
            device_id=device,
            device_id_type=MESH,
        )
        copy.start()
        sends.append(copy)
        return k

    def arrive(k, target):
        pltpu.make_async_remote_copy(
            src_ref=target,
            dst_ref=target,
            send_sem=send_sem.at[k],
            recv_sem=recv_sem.at[k],
            device_id=(slab, partner),
            device_id_type=MESH,
        ).wait_recv()

    marks = {}

    def stage_a(layer, number):
        own, ghost, lent = (
            own_bufs[layer][number],
            ghost_bufs[layer][number],
            lend_bufs[layer][number],
        )
        marks["up", layer, number] = send(lent.at[0], ghost.at[q, 0], (above, q))
        marks["down", layer, number] = send(lent.at[1], ghost.at[q, 1], (below, q))
        for j in range(1, half):
            marks["own", layer, number, j] = send(own.at[q], own.at[q], (slab, to_peer(j)))
        marks["own", layer, number, 0] = send(own.at[q], own.at[q], (slab, partner))

    def stage_b(layer, number):
        own = own_bufs[layer][number]
        for j in range(1, half):
            source = from_peer(j)
            arrive(marks["own", layer, number, j], own.at[source])
            marks["own2", layer, number, j] = send(
                own.at[source], own.at[source], (slab, partner)
            )

    def stage_c(layer, number):
        ghost = ghost_bufs[layer][number]
        arrive(marks["up", layer, number], ghost.at[q, 0])
        arrive(marks["down", layer, number], ghost.at[q, 1])
        for j in range(1, half):
            marks["ghost", layer, number, j] = send(
                ghost.at[q], ghost.at[q], (slab, to_peer(j))
            )
        marks["ghost", layer, number, 0] = send(ghost.at[q], ghost.at[q], (slab, partner))

    def stage_d(layer, number):
        ghost = ghost_bufs[layer][number]
        for j in range(1, half):
            source = from_peer(j)
            arrive(marks["ghost", layer, number, j], ghost.at[source])
            marks["ghost2", layer, number, j] = send(
                ghost.at[source], ghost.at[source], (slab, partner)
            )

    def stage_w(layer, number):
        own, ghost = own_bufs[layer][number], ghost_bufs[layer][number]
        arrive(marks["own", layer, number, 0], own.at[partner])
        arrive(marks["ghost", layer, number, 0], ghost.at[partner])
        for j in range(1, half):
            source = partner_of(from_peer(j))
            arrive(marks["own2", layer, number, j], own.at[source])
            arrive(marks["ghost2", layer, number, j], ghost.at[source])

    def table_of(layer, number):
        own, ghost = own_bufs[layer][number], ghost_bufs[layer][number]
        blocks = [own[index] for index in range(n_yz)]
        lent = [ghost[index, 0].astype(F32) for index in range(n_yz)]
        lent += [ghost[index, 1].astype(F32) for index in range(n_yz)]
        return jnp.concatenate(blocks + [jnp.concatenate(lent, axis=0).astype(BF16)], axis=0)

    def mixed(layer, number):
        table = table_of(layer, number)
        if number == 0:
            return jnp.dot(table, wv0[layer], preferred_element_type=F32).astype(BF16)
        real, imag = ((wv1, wv2), (wv3, wv4))[number - 1]
        width = table.shape[1] // 2
        stacked = jnp.concatenate([table[:, :width], table[:, width:]], axis=0)
        by_real = jnp.dot(stacked, real[layer], preferred_element_type=F32)
        by_imag = jnp.dot(stacked, imag[layer], preferred_element_type=F32)
        plus = by_real[:table_rows] - by_imag[table_rows:]
        minus = by_imag[:table_rows] + by_real[table_rows:]
        return jnp.concatenate([plus.astype(BF16), minus.astype(BF16)], axis=1)

    def compute(layer, number):
        group = groups[number]
        mix = mixed(layer, number)
        last = layer == LAYERS - 1
        for first in range(0, len(group), 2):
            places = list(range(first, min(first + 2, len(group))))
            columns = slice(places[0] * channels, (places[-1] + 1) * channels)
            gathered = jnp.dot(picks[...], mix[:, columns], preferred_element_type=F32)
            for position, place in enumerate(places):
                part = gathered[:, position * channels : (position + 1) * channels] * radp[layer]
                if last and number == 0 and place == 0:
                    for slot in range(neighb):
                        natural[pl.ds(slot, atoms, stride=neighb), :] = part[
                            slot * atoms : (slot + 1) * atoms
                        ]
                total = part.reshape(neighb, atoms, channels).sum(axis=0)
                lanes = slice(place * channels, (place + 1) * channels)
                fresh = (
                    own_bufs[layer][number][q, :, lanes].astype(F32) + 0.18 * total
                ).astype(BF16)
                if last:
                    unpacked[pl.ds(group[place], atoms, stride=stride), :] = fresh.astype(F32)
                else:
                    own_bufs[layer + 1][number][q, :, lanes] = fresh

    def permuted(store):
        for slot in range(neighb):
            store(
                slice(slot * atoms, (slot + 1) * atoms),
                natural[pl.ds(slot, atoms, stride=neighb), :],
            )

    for number in range(n_groups):
        stage_a(0, number)

    bases = radial_weight.shape[1]
    centers = 1.0 + 0.5 * lax.broadcasted_iota(jnp.int32, (bases, edges), 0).astype(F32)
    basis = jnp.exp(-jnp.square((dist[...] - centers) / 0.5)).T
    row_ids = lax.broadcasted_iota(jnp.int32, (table_rows, edges), 0)
    hot = jnp.where((row_ids == nbr[...]) & (val[...] != 0), 1.0, 0.0).astype(F32)
    scatter[:table_rows, :] = hot
    natural[...] = hot.T

    def keep_picks(rows, values):
        picks[rows, :] = values.astype(BF16)

    permuted(keep_picks)
    for layer in range(LAYERS):
        pre = jnp.dot(basis, radial_weight[layer], precision=HIGHEST, preferred_element_type=F32)
        natural[...] = pre / (1.0 + jnp.exp(-pre))

        def keep_radial(rows, values, layer=layer):
            radp[layer, rows, :] = values

        permuted(keep_radial)

    for number in range(n_groups):
        stage_b(0, number)

    atom_ids = lax.broadcasted_iota(jnp.int32, (atoms, edges), 0)
    edge_ids = lax.broadcasted_iota(jnp.int32, (atoms, edges), 1)
    mine = (edge_ids >= atom_ids * neighb) & (edge_ids < (atom_ids + 1) * neighb)
    scatter[table_rows:, :] = jnp.where(mine, 1.0, 0.0).astype(F32)
    sin_polar = jnp.sin(pol[...])
    part_ids = lax.broadcasted_iota(jnp.int32, (8, edges), 0)
    direction[...] = jnp.where(
        part_ids == 0,
        sin_polar * jnp.cos(azi[...]),
        jnp.where(
            part_ids == 1,
            sin_polar * jnp.sin(azi[...]),
            jnp.where(part_ids == 2, jnp.cos(pol[...]), 0.0),
        ),
    )

    for number in range(n_groups):
        stage_c(0, number)
    for number in range(n_groups):
        stage_d(0, number)
    for copy in weight_copies[0]:
        copy.wait()
    for number in range(n_groups):
        stage_w(0, number)
        compute(0, number)
        lend_rows(1, number)
        stage_a(1, number)
    for copy in weight_copies[1]:
        copy.wait()
    for number in range(n_groups):
        stage_b(1, number)
        stage_c(1, number)

    force_marks = []
    for number in range(n_groups):
        stage_d(1, number)
        stage_w(1, number)
        compute(1, number)
        if number == 0:
            tall = jnp.broadcast_to(readout[...], (8, channels))
            strength = 0.125 * nt_dot(tall, natural[...], HIGHEST)
            parts = nt_dot(direction[...] * strength, scatter[...], HIGHEST)
            own_force = parts[:, table_rows:]
            f_send[...] = -parts[:, :table_rows]
            for index, peer in enumerate(peers):
                force_marks.append(send(f_send, f_recv.at[index], peer))

    for atom in range(atoms):
        out_e[atom] = unpacked[stride * atom : stride * atom + coeffs, :].astype(BF16)

    table_ids = lax.broadcasted_iota(jnp.int32, (atoms, table_rows), 1)
    owner_ids = lax.broadcasted_iota(jnp.int32, (atoms, table_rows), 0)
    pick_own = table_ids == q * atoms + owner_ids
    pick_high = table_ids < 0
    pick_low = table_ids < 0
    for g in range(ghosts):
        pick_high |= (table_ids == own_rows + q * ghosts + g) & (owner_ids == send_high[g])
        pick_low |= (table_ids == own_rows + ghost_rows + q * ghosts + g) & (
            owner_ids == send_low[g]
        )
    choose = jnp.concatenate(
        [jnp.where(pick, 1.0, 0.0).astype(F32) for pick in (pick_own, pick_low, pick_high)], axis=1
    )
    for index, k in enumerate(force_marks):
        arrive(k, f_recv.at[index])
    own_sum = f_send[...]
    for index in range(n_yz - 1):
        own_sum = own_sum + f_recv[index]
    below_sum = f_recv[n_yz - 1]
    above_sum = f_recv[2 * n_yz - 1]
    for index in range(1, n_yz):
        below_sum = below_sum + f_recv[n_yz - 1 + index]
        above_sum = above_sum + f_recv[2 * n_yz - 1 + index]
    gathered = jnp.concatenate([own_sum, below_sum, above_sum], axis=1)
    out_f[...] = (own_force + nt_dot(gathered, choose, HIGHEST))[:3]

    for copy in sends:
        copy.wait_send()


def body(
    n_slab,
    n_yz,
    embeddings,
    neighbours,
    valid,
    azimuth,
    polar,
    distance,
    send_low,
    send_high,
    w_zero,
    w_one_re,
    w_one_im,
    w_two_re,
    w_two_im,
    radial_weight,
    readout,
):
    atoms, coeffs, channels = embeddings.shape
    degrees = math.isqrt(coeffs)
    edges = neighbours.shape[0]
    neighb = edges // atoms
    ghosts = send_low.shape[0]
    stride = (coeffs + 7) // 8 * 8
    groups = slot_groups(degrees)
    table_rows = n_yz * (atoms + 2 * ghosts)
    widths = [len(group) * channels for group in groups]
    weights = (w_zero, w_one_re, w_one_im, w_two_re, w_two_im)
    n_peers = 3 * n_yz - 1
    half = n_yz // 2
    copies = LAYERS * len(groups) * (2 + 2 * half + 2 * (half - 1)) + n_peers
    vmem = pl.BlockSpec(memory_space=pltpu.VMEM)
    smem = pl.BlockSpec(memory_space=pltpu.SMEM)
    hbm = pl.BlockSpec(memory_space=pl.ANY)
    row = lambda array: array.reshape(1, edges)
    scratch = [pltpu.VMEM(weight.shape, BF16) for weight in weights]
    scratch += [
        pltpu.VMEM((atoms * stride, channels), F32),
        pltpu.VMEM((edges, channels), F32),
        pltpu.VMEM((LAYERS, edges, channels), F32),
        pltpu.VMEM((edges, table_rows), BF16),
        pltpu.VMEM((table_rows + atoms, edges), F32),
        pltpu.VMEM((8, edges), F32),
        pltpu.VMEM((8, table_rows), F32),
        pltpu.VMEM((n_peers, 8, table_rows), F32),
    ]
    for _ in range(LAYERS):
        scratch += [pltpu.VMEM((n_yz, atoms, width), BF16) for width in widths]
    for _ in range(LAYERS):
        scratch += [pltpu.VMEM((n_yz, 2, ghosts, width), BF16) for width in widths]
    for _ in range(LAYERS):
        scratch += [pltpu.VMEM((2, ghosts, width), BF16) for width in widths]
    scratch += [
        pltpu.SemaphoreType.DMA((5 * LAYERS,)),
        pltpu.SemaphoreType.DMA((copies,)),
        pltpu.SemaphoreType.DMA((copies,)),
    ]
    return pl.pallas_call(
        functools.partial(
            kernel, n_slab, n_yz, atoms, coeffs, stride, channels, ghosts, neighb, groups
        ),
        out_shape=(
            jax.ShapeDtypeStruct(embeddings.shape, BF16),
            jax.ShapeDtypeStruct((3, atoms), F32),
        ),
        in_specs=[vmem] * 6 + [smem] * 2 + [hbm] * 5 + [vmem] * 2,
        out_specs=(vmem, vmem),
        scratch_shapes=scratch,
        compiler_params=pltpu.CompilerParams(collective_id=0, has_side_effects=True),
    )(
        embeddings,
        row(neighbours),
        row(valid),
        row(azimuth),
        row(polar),
        row(distance),
        send_low,
        send_high,
        *weights,
        radial_weight,
        readout.reshape(1, channels),
    )


def solution(mesh):
    both = ("slab", "yz")
    in_specs = (P(both, None, None),) + (P(both),) * 7 + (P(),) * 7
    out_specs = (P(both, None, None), P(None, both))
    return jax.shard_map(
        functools.partial(body, mesh.shape["slab"], mesh.shape["yz"]),
        mesh=mesh,
        in_specs=in_specs,
        out_specs=out_specs,
        check_vma=False,
    )
```

time: 161 us -> 36.5 us (0.23)
  blocking collectives: 43.3 us -> 0 us
  local copies, waits for them, and re-layouts: 38.6 us -> 4.41 us
  matrix products: 34.1 us -> 0 us
  Pallas kernels: 0 us -> 31.3 us
  between operations: 15.8 us -> 0.64 us
  other arithmetic: 14 us -> 0 us
  starting transfers between devices: 13 us -> 0 us
    all_gather x6 -> x0, blocking collectives: 36.8 us -> none  [the longest x2 13.6 us: body(): lax.all_gather(outgoing, 'yz', axis=0, tiled=True)]
    dot_general x24 -> x0, matrix products: 34.1 us -> none  [the longest x4 10.3 us: convolve(): jnp.dot(turned_minus, real_part, preferred_element_type=jnp.float32)]
    pallas_call x0 -> x1, Pallas kernels: none -> 31.3 us  [body(): pl.pallas_call(functools.partial(kernel, n_slab, n_yz, atoms, coeffs, str...]
    reshape x8 -> x0, local copies, waits for them, and re-layouts: 14.6 us -> none  [the longest x4 7.79 us: convolve(): out_minus = (jnp.dot(turned_plus, imag_part, preferred_element_type=jnp.f...]
    ppermute x6 -> x0, starting transfers between devices: 12.9 us -> none  [from_behind(): return lax.ppermute(block, axis, route)]
    reduce_sum x5 -> x0, other arithmetic: 11.3 us -> none  [the longest x4 11.3 us: convolve(): back_plus = (cos_rows * out_plus - sin_rows * out_minus).reshape(atom_cou...]
    gather x6 -> x0, local copies, waits for them, and re-layouts: 9.93 us -> none  [the longest x2 5.22 us: body(): table[neighbours]]
    unnamed x1 -> x0, blocking collectives: 6.48 us -> none
  transfers between devices with their start and end apart: 7 -> 0, of which waited for: 1 -> 0; matrix products, arithmetic and copies ran while one was open for 24% -> 0% of each run, Pallas kernels for 0% -> 0%
where the time goes in v1:
time: 36.5 us; the launch traced here: 36.3 us
  Pallas kernels  31.3 us (86%)
  local copies, waits for them, and re-layouts  4.41 us (12%)
  between operations  0.64 us (2%)
    pallas_call x1, Pallas kernels, body(): pl.pallas_call(functools.partial(kernel, n_slab, n_yz, atoms, coeffs, str...  31.3 us
    unnamed x2, local copies, waits for them, and re-layouts  2.83 us
    pallas_call x1, local copies, waits for them, and re-layouts, body(): pl.pallas_call(functools.partial(kernel, n_slab, n_yz, atoms, coeffs, str...  1.59 us

profile of v1, /device:TPU:0, one launch (start us, length us, event | category | flops | bytes accessed | tf_op | source)
XLA Modules:
  0.0 36.3 jit_solution(4059171331623928340)
XLA Ops:
  0.6 1.6 %copy.17.emb = bf16[16,25,128]{2,1,0:T(8,128)(2,1)} copy(bf16[16,25,128]{2,0,1:T(8,128)(2,1)} %param.15) | data formatting | bytes 204800 | tf_op args[0]
  2.2 31.3 %shard_map.158 = (bf16[16,25,128]{2,1,0:T(8,128)(2,1)}, f32[3,16]{1,0:T(4,128)}) custom-call(bf16[16,25,128]{2,1,0:T(8,128)(2,1)} %copy.17.emb, s32[1,512]{1,0:T(1,128)} %bitcast.6, s32[1,512]{1,0:T(1,128)} %bitcast.7, f32[1,512]{1,0:T(1,128)} %bitcast.8, f32[1,512]{1,0:T(1,128)} %bitcast.9, f32[1,512]{1,0:T(1,128)} %bitcast.10, s32[8]{0:T(128)} %send_low.1, ...), custom_call_target="tpu_custom_call" | custom-call | tf_op jit(solution)/shard_map/pallas_call | solution.py:453
  33.5 1.6 %copy.18 = bf16[16,25,128]{2,0,1:T(8,128)(2,1)} copy(bf16[16,25,128]{2,1,0:T(8,128)(2,1)} %get-tuple-element.2) | data formatting | bytes 204800 | tf_op jit(solution)/shard_map/pallas_call | solution.py:453
  35.1 1.2 %copy.20 = f32[3,16]{1,0:T(4,128)} copy(f32[3,16]{1,0:T(4,128)} %get-tuple-element.7) | data formatting | bytes 384

commit v2 on v1

--- a/solution.py
+++ b/solution.py
@@ -40,7 +40,6 @@
     n_yz,
     atoms,
     coeffs,
-    stride,
     channels,
     ghosts,
     neighb,
@@ -67,7 +66,6 @@
     wv2,
     wv3,
     wv4,
-    unpacked,
     natural,
     radp,
     picks,
@@ -143,13 +141,9 @@
         lend_bufs[layer][number][0] = rows[:ghosts].astype(BF16)
         lend_bufs[layer][number][1] = rows[ghosts:].astype(BF16)
 
-    for atom in range(atoms):
-        unpacked[stride * atom : stride * atom + coeffs, :] = emb[atom].astype(F32)
     for number, group in enumerate(groups):
         for place, slot in enumerate(group):
-            own_bufs[0][number][q, :, place * channels : (place + 1) * channels] = unpacked[
-                pl.ds(slot, atoms, stride=stride), :
-            ].astype(BF16)
+            own_bufs[0][number][q, :, place * channels : (place + 1) * channels] = emb[slot]
         lend_rows(0, number)
 
     pl.semaphore_wait(barrier, len(peers))
@@ -274,7 +268,7 @@
                     own_bufs[layer][number][q, :, lanes].astype(F32) + 0.18 * total
                 ).astype(BF16)
                 if last:
-                    unpacked[pl.ds(group[place], atoms, stride=stride), :] = fresh.astype(F32)
+                    out_e[group[place]] = fresh
                 else:
                     own_bufs[layer + 1][number][q, :, lanes] = fresh
 
@@ -359,8 +353,9 @@
             for index, peer in enumerate(peers):
                 force_marks.append(send(f_send, f_recv.at[index], peer))
 
-    for atom in range(atoms):
-        out_e[atom] = unpacked[stride * atom : stride * atom + coeffs, :].astype(BF16)
+    for slot in range(coeffs):
+        if not any(slot in group for group in groups):
+            out_e[slot] = emb[slot]
 
     table_ids = lax.broadcasted_iota(jnp.int32, (atoms, table_rows), 1)
     owner_ids = lax.broadcasted_iota(jnp.int32, (atoms, table_rows), 0)
@@ -416,7 +411,6 @@
     edges = neighbours.shape[0]
     neighb = edges // atoms
     ghosts = send_low.shape[0]
-    stride = (coeffs + 7) // 8 * 8
     groups = slot_groups(degrees)
     table_rows = n_yz * (atoms + 2 * ghosts)
     widths = [len(group) * channels for group in groups]
@@ -430,7 +424,6 @@
     row = lambda array: array.reshape(1, edges)
     scratch = [pltpu.VMEM(weight.shape, BF16) for weight in weights]
     scratch += [
-        pltpu.VMEM((atoms * stride, channels), F32),
         pltpu.VMEM((edges, channels), F32),
         pltpu.VMEM((LAYERS, edges, channels), F32),
         pltpu.VMEM((edges, table_rows), BF16),
@@ -450,12 +443,12 @@
         pltpu.SemaphoreType.DMA((copies,)),
         pltpu.SemaphoreType.DMA((copies,)),
     ]
-    return pl.pallas_call(
+    updated, forces = pl.pallas_call(
         functools.partial(
-            kernel, n_slab, n_yz, atoms, coeffs, stride, channels, ghosts, neighb, groups
+            kernel, n_slab, n_yz, atoms, coeffs, channels, ghosts, neighb, groups
         ),
         out_shape=(
-            jax.ShapeDtypeStruct(embeddings.shape, BF16),
+            jax.ShapeDtypeStruct((coeffs, atoms, channels), BF16),
             jax.ShapeDtypeStruct((3, atoms), F32),
         ),
         in_specs=[vmem] * 6 + [smem] * 2 + [hbm] * 5 + [vmem] * 2,
@@ -463,7 +456,7 @@
         scratch_shapes=scratch,
         compiler_params=pltpu.CompilerParams(collective_id=0, has_side_effects=True),
     )(
-        embeddings,
+        jnp.transpose(embeddings, (1, 0, 2)),
         row(neighbours),
         row(valid),
         row(azimuth),
@@ -475,6 +468,7 @@
         radial_weight,
         readout.reshape(1, channels),
     )
+    return (jnp.transpose(updated, (1, 0, 2)), forces)
 
 
 def solution(mesh):

time: 36.5 us -> 34.9 us (0.956)
  local copies, waits for them, and re-layouts: 4.41 us -> 2.79 us
    pallas_call x1 -> x0, local copies, waits for them, and re-layouts: 1.59 us -> none  [body(): pl.pallas_call(functools.partial(kernel, n_slab, n_yz, atoms, coeffs, str...]
where the time goes in v2:
time: 34.9 us; the launch traced here: 34.7 us
  Pallas kernels  31.2 us (89%)
  local copies, waits for them, and re-layouts  2.79 us (8%)
  between operations  0.64 us (2%)
    pallas_call x1, Pallas kernels, body(): pl.pallas_call(functools.partial(kernel, n_slab, n_yz, atoms, coeffs, cha...  31.2 us
    unnamed x2, local copies, waits for them, and re-layouts  2.79 us

profile of v2, /device:TPU:0, one launch (start us, length us, event | category | flops | bytes accessed | tf_op | source)
XLA Modules:
  0.0 34.7 jit_solution(2455043802476389323)
XLA Ops:
  0.6 31.2 %shard_map.158 = (bf16[25,16,128]{2,1,0:T(8,128)(2,1)}, f32[3,16]{1,0:T(4,128)}) custom-call(bf16[25,16,128]{2,1,0:T(8,128)(2,1)} %bitcast.8, s32[1,512]{1,0:T(1,128)} %bitcast.10, s32[1,512]{1,0:T(1,128)} %bitcast.11, f32[1,512]{1,0:T(1,128)} %bitcast.12, f32[1,512]{1,0:T(1,128)} %bitcast.13, f32[1,512]{1,0:T(1,128)} %bitcast.14, s32[8]{0:T(128)} %send_low.1, ...), custom_call_target="tpu_custom_call" | custom-call | tf_op jit(solution)/shard_map/pallas_call | solution.py:446
  31.9 1.5 %copy.19 = bf16[16,25,128]{2,0,1:T(8,128)(2,1)} copy(bf16[16,25,128]{2,0,1:T(8,128)(2,1)} %bitcast.9) | data formatting | bytes 204800
  33.4 1.2 %copy.20 = f32[3,16]{1,0:T(4,128)} copy(f32[3,16]{1,0:T(4,128)} %get-tuple-element.9) | data formatting | bytes 384

commit v3 on v2

--- a/solution.py
+++ b/solution.py
@@ -33,6 +33,19 @@
     return lax.dot_general(
         left, right, (((1,), (1,)), ((), ())), precision=precision, preferred_element_type=F32
     )
+
+
+def thirds(values):
+    head = values.astype(BF16).astype(F32)
+    mid = (values - head).astype(BF16).astype(F32)
+    return head, mid, values - head - mid
+
+
+def thirds_dot(values, exact):
+    rows = jnp.concatenate(thirds(values), axis=0).astype(BF16)
+    total = nt_dot(rows, exact)
+    count = values.shape[0]
+    return total[:count] + (total[count : 2 * count] + total[2 * count :])
 
 
 def kernel(
@@ -71,6 +84,8 @@
     picks,
     scatter,
     direction,
+    chooser,
+    fresh_e,
     f_send,
     f_recv,
     *rest,
@@ -82,7 +97,7 @@
     rest = rest[LAYERS * n_groups :]
     lend_bufs = [rest[layer * n_groups : (layer + 1) * n_groups] for layer in range(LAYERS)]
     rest = rest[LAYERS * n_groups :]
-    weight_sem, send_sem, recv_sem = rest
+    weight_sem, out_sem, send_sem, recv_sem = rest
 
     edges = atoms * neighb
     own_rows = n_yz * atoms
@@ -268,7 +283,7 @@
                     own_bufs[layer][number][q, :, lanes].astype(F32) + 0.18 * total
                 ).astype(BF16)
                 if last:
-                    out_e[group[place]] = fresh
+                    fresh_e[group[place]] = fresh
                 else:
                     own_bufs[layer + 1][number][q, :, lanes] = fresh
 
@@ -287,7 +302,7 @@
     basis = jnp.exp(-jnp.square((dist[...] - centers) / 0.5)).T
     row_ids = lax.broadcasted_iota(jnp.int32, (table_rows, edges), 0)
     hot = jnp.where((row_ids == nbr[...]) & (val[...] != 0), 1.0, 0.0).astype(F32)
-    scatter[:table_rows, :] = hot
+    scatter[:table_rows, :] = hot.astype(BF16)
     natural[...] = hot.T
 
     def keep_picks(rows, values):
@@ -309,7 +324,7 @@
     atom_ids = lax.broadcasted_iota(jnp.int32, (atoms, edges), 0)
     edge_ids = lax.broadcasted_iota(jnp.int32, (atoms, edges), 1)
     mine = (edge_ids >= atom_ids * neighb) & (edge_ids < (atom_ids + 1) * neighb)
-    scatter[table_rows:, :] = jnp.where(mine, 1.0, 0.0).astype(F32)
+    scatter[table_rows:, :] = jnp.where(mine, 1.0, 0.0).astype(F32).astype(BF16)
     sin_polar = jnp.sin(pol[...])
     part_ids = lax.broadcasted_iota(jnp.int32, (8, edges), 0)
     direction[...] = jnp.where(
@@ -322,6 +337,27 @@
         ),
     )
 
+    table_ids = lax.broadcasted_iota(jnp.int32, (atoms, table_rows), 1)
+    owner_ids = lax.broadcasted_iota(jnp.int32, (atoms, table_rows), 0)
+    pick = table_ids == q * atoms + owner_ids
+    for g in range(ghosts):
+        pick |= (table_ids == own_rows + q * ghosts + g) & (owner_ids == send_high[g])
+        pick |= (table_ids == own_rows + ghost_rows + q * ghosts + g) & (
+            owner_ids == send_low[g]
+        )
+    chooser[...] = jnp.where(pick, 1.0, 0.0).astype(F32).astype(BF16)
+
+    out_copies = []
+
+    def write_out(source, slots):
+        for slot in slots:
+            copy = pltpu.make_async_copy(source.at[slot], out_e.at[slot], out_sem.at[slot])
+            copy.start()
+            out_copies.append(copy)
+
+    used = {slot for group in groups for slot in group}
+    write_out(emb, [slot for slot in range(coeffs) if slot not in used])
+
     for number in range(n_groups):
         stage_c(0, number)
     for number in range(n_groups):
@@ -342,34 +378,25 @@
     force_marks = []
     for number in range(n_groups):
         stage_d(1, number)
+    for number in range(n_groups):
         stage_w(1, number)
         compute(1, number)
+        write_out(fresh_e, groups[number])
         if number == 0:
             tall = jnp.broadcast_to(readout[...], (8, channels))
-            strength = 0.125 * nt_dot(tall, natural[...], HIGHEST)
-            parts = nt_dot(direction[...] * strength, scatter[...], HIGHEST)
+            tall_head, tall_mid, tall_tail = thirds(tall)
+            tall_rows = jnp.concatenate([tall_head, tall_mid, tall_tail], axis=0).astype(BF16)
+            scalar_head, scalar_mid, scalar_tail = thirds(natural[...])
+            total = nt_dot(tall_rows, scalar_head.astype(BF16))
+            total += nt_dot(tall_rows, scalar_mid.astype(BF16))
+            total += nt_dot(tall_rows, scalar_tail.astype(BF16))
+            strength = 0.125 * (total[:8] + (total[8:16] + total[16:24]))
+            parts = thirds_dot(direction[...] * strength, scatter[...])
             own_force = parts[:, table_rows:]
             f_send[...] = -parts[:, :table_rows]
             for index, peer in enumerate(peers):
                 force_marks.append(send(f_send, f_recv.at[index], peer))
 
-    for slot in range(coeffs):
-        if not any(slot in group for group in groups):
-            out_e[slot] = emb[slot]
-
-    table_ids = lax.broadcasted_iota(jnp.int32, (atoms, table_rows), 1)
-    owner_ids = lax.broadcasted_iota(jnp.int32, (atoms, table_rows), 0)
-    pick_own = table_ids == q * atoms + owner_ids
-    pick_high = table_ids < 0
-    pick_low = table_ids < 0
-    for g in range(ghosts):
-        pick_high |= (table_ids == own_rows + q * ghosts + g) & (owner_ids == send_high[g])
-        pick_low |= (table_ids == own_rows + ghost_rows + q * ghosts + g) & (
-            owner_ids == send_low[g]
-        )
-    choose = jnp.concatenate(
-        [jnp.where(pick, 1.0, 0.0).astype(F32) for pick in (pick_own, pick_low, pick_high)], axis=1
-    )
     for index, k in enumerate(force_marks):
         arrive(k, f_recv.at[index])
     own_sum = f_send[...]
@@ -380,11 +407,23 @@
     for index in range(1, n_yz):
         below_sum = below_sum + f_recv[n_yz - 1 + index]
         above_sum = above_sum + f_recv[2 * n_yz - 1 + index]
-    gathered = jnp.concatenate([own_sum, below_sum, above_sum], axis=1)
-    out_f[...] = (own_force + nt_dot(gathered, choose, HIGHEST))[:3]
-
+    lane = lax.broadcasted_iota(jnp.int32, (8, table_rows), 1)
+    returned = jnp.where(
+        lane < own_rows,
+        own_sum,
+        jnp.where(lane < own_rows + ghost_rows, above_sum, below_sum),
+    )
+    out_f[...] = (own_force + thirds_dot(returned, chooser[...]))[:3]
+
+    for copy in out_copies:
+        copy.wait()
     for copy in sends:
         copy.wait_send()
+
+
+def hand_over(rows, forces, rows_out, forces_out):
+    rows_out[...] = rows[...]
+    forces_out[...] = forces[...]
 
 
 def body(
@@ -427,8 +466,10 @@
         pltpu.VMEM((edges, channels), F32),
         pltpu.VMEM((LAYERS, edges, channels), F32),
         pltpu.VMEM((edges, table_rows), BF16),
-        pltpu.VMEM((table_rows + atoms, edges), F32),
+        pltpu.VMEM((table_rows + atoms, edges), BF16),
         pltpu.VMEM((8, edges), F32),
+        pltpu.VMEM((atoms, table_rows), BF16),
+        pltpu.VMEM((coeffs, atoms, channels), BF16),
         pltpu.VMEM((8, table_rows), F32),
         pltpu.VMEM((n_peers, 8, table_rows), F32),
     ]
@@ -440,6 +481,7 @@
         scratch += [pltpu.VMEM((2, ghosts, width), BF16) for width in widths]
     scratch += [
         pltpu.SemaphoreType.DMA((5 * LAYERS,)),
+        pltpu.SemaphoreType.DMA((coeffs,)),
         pltpu.SemaphoreType.DMA((copies,)),
         pltpu.SemaphoreType.DMA((copies,)),
     ]
@@ -452,7 +494,7 @@
             jax.ShapeDtypeStruct((3, atoms), F32),
         ),
         in_specs=[vmem] * 6 + [smem] * 2 + [hbm] * 5 + [vmem] * 2,
-        out_specs=(vmem, vmem),
+        out_specs=(hbm, vmem),
         scratch_shapes=scratch,
         compiler_params=pltpu.CompilerParams(collective_id=0, has_side_effects=True),
     )(
@@ -468,6 +510,15 @@
         radial_weight,
         readout.reshape(1, channels),
     )
+    updated, forces = pl.pallas_call(
+        hand_over,
+        out_shape=(
+            jax.ShapeDtypeStruct(updated.shape, BF16),
+            jax.ShapeDtypeStruct(forces.shape, F32),
+        ),
+        in_specs=[vmem, vmem],
+        out_specs=(vmem, vmem),
+    )(updated, forces)
     return (jnp.transpose(updated, (1, 0, 2)), forces)
 
 

time: 34.9 us -> 35 us (level)
  Pallas kernels: 31.2 us -> 34.1 us
  local copies, waits for them, and re-layouts: 2.79 us -> 0 us
    unnamed x2 -> x0, local copies, waits for them, and re-layouts: 2.79 us -> none
    pallas_call x0 -> x1, Pallas kernels: none -> 1.55 us  [body(): pl.pallas_call(hand_over, out_shape=(jax.ShapeDtypeStruct(updated.shape,...]
    pallas_call x1, Pallas kernels: 31.2 us -> 32.6 us  [body(): pl.pallas_call(functools.partial(kernel, n_slab, n_yz, atoms, coeffs, cha...]
where the time goes in v3:
time: 35 us; the launch traced here: 34.8 us
  Pallas kernels  34.1 us (97%)
  between operations  0.64 us (2%)
    pallas_call x1, Pallas kernels, body(): pl.pallas_call(functools.partial(kernel, n_slab, n_yz, atoms, coeffs, cha...  32.6 us
    pallas_call x1, Pallas kernels, body(): pl.pallas_call(hand_over, out_shape=(jax.ShapeDtypeStruct(updated.shape,...  1.55 us

profile of v3, /device:TPU:0, one launch (start us, length us, event | category | flops | bytes accessed | tf_op | source)
XLA Modules:
  0.0 34.8 jit_solution(9754291297968075523)
XLA Ops:
  0.6 32.6 %shard_map.158 = (bf16[25,16,128]{2,1,0:T(8,128)(2,1)}, f32[3,16]{1,0:T(4,128)}) custom-call(bf16[25,16,128]{2,1,0:T(8,128)(2,1)} %bitcast.8, s32[1,512]{1,0:T(1,128)} %bitcast.9, s32[1,512]{1,0:T(1,128)} %bitcast.10, f32[1,512]{1,0:T(1,128)} %bitcast.11, f32[1,512]{1,0:T(1,128)} %bitcast.12, f32[1,512]{1,0:T(1,128)} %bitcast.13, s32[8]{0:T(128)} %send_low.1, ...), custom_call_target="tpu_custom_call" | custom-call | tf_op jit(solution)/shard_map/pallas_call | solution.py:488
  33.2 1.5 %shard_map.159 = (bf16[25,16,128]{2,1,0:T(8,128)(2,1)}, f32[3,16]{1,0:T(4,128)}) custom-call(bf16[25,16,128]{2,1,0:T(8,128)(2,1)} %get-tuple-element.6.rows, f32[3,16]{1,0:T(4,128)} %get-tuple-element.7.forces), custom_call_target="tpu_custom_call" | custom-call | tf_op jit(solution)/shard_map/pallas_call | solution.py:513

commit v4 on v3

--- a/solution.py
+++ b/solution.py
@@ -85,7 +85,6 @@
     scatter,
     direction,
     chooser,
-    fresh_e,
     f_send,
     f_recv,
     *rest,
@@ -97,7 +96,7 @@
     rest = rest[LAYERS * n_groups :]
     lend_bufs = [rest[layer * n_groups : (layer + 1) * n_groups] for layer in range(LAYERS)]
     rest = rest[LAYERS * n_groups :]
-    weight_sem, out_sem, send_sem, recv_sem = rest
+    weight_sem, send_sem, recv_sem = rest
 
     edges = atoms * neighb
     own_rows = n_yz * atoms
@@ -283,7 +282,7 @@
                     own_bufs[layer][number][q, :, lanes].astype(F32) + 0.18 * total
                 ).astype(BF16)
                 if last:
-                    fresh_e[group[place]] = fresh
+                    out_e[group[place]] = fresh
                 else:
                     own_bufs[layer + 1][number][q, :, lanes] = fresh
 
@@ -347,16 +346,10 @@
         )
     chooser[...] = jnp.where(pick, 1.0, 0.0).astype(F32).astype(BF16)
 
-    out_copies = []
-
-    def write_out(source, slots):
-        for slot in slots:
-            copy = pltpu.make_async_copy(source.at[slot], out_e.at[slot], out_sem.at[slot])
-            copy.start()
-            out_copies.append(copy)
-
     used = {slot for group in groups for slot in group}
-    write_out(emb, [slot for slot in range(coeffs) if slot not in used])
+    for slot in range(coeffs):
+        if slot not in used:
+            out_e[slot] = emb[slot]
 
     for number in range(n_groups):
         stage_c(0, number)
@@ -375,13 +368,12 @@
         stage_b(1, number)
         stage_c(1, number)
 
-    force_marks = []
+    force_marks = {}
     for number in range(n_groups):
         stage_d(1, number)
     for number in range(n_groups):
         stage_w(1, number)
         compute(1, number)
-        write_out(fresh_e, groups[number])
         if number == 0:
             tall = jnp.broadcast_to(readout[...], (8, channels))
             tall_head, tall_mid, tall_tail = thirds(tall)
@@ -394,10 +386,11 @@
             parts = thirds_dot(direction[...] * strength, scatter[...])
             own_force = parts[:, table_rows:]
             f_send[...] = -parts[:, :table_rows]
-            for index, peer in enumerate(peers):
-                force_marks.append(send(f_send, f_recv.at[index], peer))
-
-    for index, k in enumerate(force_marks):
+            order = list(range(n_yz - 1, len(peers))) + list(range(n_yz - 1))
+            for index in order:
+                force_marks[index] = send(f_send, f_recv.at[index], peers[index])
+
+    for index, k in force_marks.items():
         arrive(k, f_recv.at[index])
     own_sum = f_send[...]
     for index in range(n_yz - 1):
@@ -415,8 +408,6 @@
     )
     out_f[...] = (own_force + thirds_dot(returned, chooser[...]))[:3]
 
-    for copy in out_copies:
-        copy.wait()
     for copy in sends:
         copy.wait_send()
 
@@ -469,7 +460,6 @@
         pltpu.VMEM((table_rows + atoms, edges), BF16),
         pltpu.VMEM((8, edges), F32),
         pltpu.VMEM((atoms, table_rows), BF16),
-        pltpu.VMEM((coeffs, atoms, channels), BF16),
         pltpu.VMEM((8, table_rows), F32),
         pltpu.VMEM((n_peers, 8, table_rows), F32),
     ]
@@ -481,7 +471,6 @@
         scratch += [pltpu.VMEM((2, ghosts, width), BF16) for width in widths]
     scratch += [
         pltpu.SemaphoreType.DMA((5 * LAYERS,)),
-        pltpu.SemaphoreType.DMA((coeffs,)),
         pltpu.SemaphoreType.DMA((copies,)),
         pltpu.SemaphoreType.DMA((copies,)),
     ]
@@ -490,11 +479,11 @@
             kernel, n_slab, n_yz, atoms, coeffs, channels, ghosts, neighb, groups
         ),
         out_shape=(
-            jax.ShapeDtypeStruct((coeffs, atoms, channels), BF16),
-            jax.ShapeDtypeStruct((3, atoms), F32),
+            pltpu.VMEM((coeffs, atoms, channels), BF16),
+            pltpu.VMEM((3, atoms), F32),
         ),
         in_specs=[vmem] * 6 + [smem] * 2 + [hbm] * 5 + [vmem] * 2,
-        out_specs=(hbm, vmem),
+        out_specs=(vmem, vmem),
         scratch_shapes=scratch,
         compiler_params=pltpu.CompilerParams(collective_id=0, has_side_effects=True),
     )(
@@ -518,7 +507,10 @@
         ),
         in_specs=[vmem, vmem],
         out_specs=(vmem, vmem),
-    )(updated, forces)
+    )(
+        pltpu.with_memory_space_constraint(updated, pltpu.VMEM),
+        pltpu.with_memory_space_constraint(forces, pltpu.VMEM),
+    )
     return (jnp.transpose(updated, (1, 0, 2)), forces)
 
 

time: 35 us -> 33.2 us (0.949)
  Pallas kernels: 34.1 us -> 32.4 us
    pallas_call x1, Pallas kernels: 1.55 us -> 0.65 us  [body(): pl.pallas_call(hand_over, out_shape=(jax.ShapeDtypeStruct(updated.shape,...]
    pallas_call x1, Pallas kernels: 32.6 us -> 31.7 us  [body(): pl.pallas_call(functools.partial(kernel, n_slab, n_yz, atoms, coeffs, cha...]
where the time goes in v4:
time: 33.2 us; the launch traced here: 33 us
  Pallas kernels  32.4 us (98%)
  between operations  0.64 us (2%)
    pallas_call x1, Pallas kernels, body(): pl.pallas_call(functools.partial(kernel, n_slab, n_yz, atoms, coeffs, cha...  31.7 us

profile of v4, /device:TPU:0, one launch (start us, length us, event | category | flops | bytes accessed | tf_op | source)
XLA Modules:
  0.0 33.0 jit_solution(15284561159914766003)
XLA Ops:
  0.6 31.7 %shard_map.158 = (bf16[25,16,128]{2,1,0:T(8,128)(2,1)S(1)}, f32[3,16]{1,0:T(4,128)S(1)}) custom-call(bf16[25,16,128]{2,1,0:T(8,128)(2,1)} %bitcast.8, s32[1,512]{1,0:T(1,128)} %bitcast.9, s32[1,512]{1,0:T(1,128)} %bitcast.10, f32[1,512]{1,0:T(1,128)} %bitcast.11, f32[1,512]{1,0:T(1,128)} %bitcast.12, f32[1,512]{1,0:T(1,128)} %bitcast.13, s32[8]{0:T(128)} %send_low.1, ...), custom_call_target="tpu_custom_call" | custom-call | tf_op jit(solution)/shard_map/pallas_call | solution.py:477
  32.4 0.7 %shard_map.159 = (bf16[25,16,128]{2,1,0:T(8,128)(2,1)}, f32[3,16]{1,0:T(4,128)}) custom-call(bf16[25,16,128]{2,1,0:T(8,128)(2,1)S(1)} %get-tuple-element.6.rows, f32[3,16]{1,0:T(4,128)S(1)} %get-tuple-element.7.forces), custom_call_target="tpu_custom_call" | custom-call | tf_op jit(solution)/shard_map/pallas_call | solution.py:502
